TPU v7x, 32 devices: a whole 2x2x4 slice. The times are simulated.
32 devices in a mesh: seq: 8 (over z, x), exp: 4 (over y, core).
Axes of the slice: x: 2, y: 2, z: 4, core: 2. Of those that a mesh axis runs over, the one named last changes fastest.
Arguments:
- tokens: bfloat16 [4, 1024, 4096], P('exp', 'seq'), may hold values from -6 to 6
- out_grad: bfloat16 [4, 1024, 4096], P('exp', 'seq'), may hold values from -0.59765625 to 0.59765625
- router_weight: bfloat16 [4096, 32], replicated, may hold values from -8 to 8
- gate_weight: bfloat16 [32, 4096, 768], P(('seq', 'exp')), may hold values from -0.09375 to 0.09375
- up_weight: bfloat16 [32, 4096, 768], P(('seq', 'exp')), may hold values from -0.09375 to 0.09375
- down_weight: bfloat16 [32, 768, 4096], P(('seq', 'exp')), may hold values from -0.21875 to 0.21875
- saved_gate: bfloat16 [32, 2048, 768], P(('seq', 'exp')), may hold values from -6 to 6
- saved_up: bfloat16 [32, 2048, 768], P(('seq', 'exp')), may hold values from -6 to 6
- expert_ids: int32 [4, 1024, 8], P('exp', 'seq'), may hold values from 0 to 31, as said below
- aux_weight: float32 [1], replicated, may hold values from 2 to 6
Outputs:
- token_grad: bfloat16 [4, 1024, 4096], P('exp', 'seq')
- combine_grad: float32 [4, 1024, 8], P('exp', 'seq')
- router_grad: float32 [4096, 32], P(('seq', 'exp'))
Inputs may be any that keep to these rules, and one draw needn't show every extreme that they name: `expert_ids`: among the rows of one device (128 tokens) each expert is named at most 64 times, and some expert exactly 64 times; a token's 8 experts differ.
All inputs are finite; a program needn't handle non-finite values.
Results may differ from a plain program's by a relative error of at most 0.013.
Values may be sent and summed in bfloat16 or wider, within the bound.
A program may use at most 192 MiB of HBM per device.

v0:
```python
import jax
import jax.numpy as jnp
from jax import lax
from jax.sharding import PartitionSpec as P


def expert_backward(grad_rows, gate_rows, w_gate, w_up, w_down, pre_gate, pre_up):
    upstream = jnp.einsum("rd,fd->rf", grad_rows, w_down, preferred_element_type=jnp.float32)
    first = pre_gate.astype(jnp.float32)
    second = pre_up.astype(jnp.float32)
    gate_sig = jax.nn.sigmoid(first)
    gate_act = first * gate_sig
    hidden = gate_act * second
    slot_combine = jnp.sum(upstream * hidden, axis=-1).astype(jnp.bfloat16)
    scaled = gate_rows.astype(jnp.float32)[:, None] * upstream
    grad_first = (scaled * second * gate_sig * (1.0 + first * (1.0 - gate_sig))).astype(
        jnp.bfloat16
    )
    grad_second = (scaled * gate_act).astype(jnp.bfloat16)
    back_rows = jnp.einsum("rf,df->rd", grad_first, w_gate, preferred_element_type=jnp.float32)
    back_rows = back_rows + jnp.einsum(
        "rf,df->rd", grad_second, w_up, preferred_element_type=jnp.float32
    )
    return (back_rows.astype(jnp.bfloat16), slot_combine)


def shards(
    tokens,
    out_grad,
    router_weight,
    gate_weight,
    up_weight,
    down_weight,
    saved_gate,
    saved_up,
    expert_ids,
    aux_weight,
):
    seq_size = lax.axis_size("seq")
    exp_size = lax.axis_size("exp")
    devices = seq_size * exp_size
    inputs = tokens[0]
    upstream_grad = out_grad[0]
    chosen_ids = expert_ids[0]
    tok_rows, top_count = chosen_ids.shape
    model_width = inputs.shape[1]
    experts = router_weight.shape[1]
    capacity = saved_gate.shape[1] // devices
    logits = jnp.dot(inputs, router_weight, preferred_element_type=jnp.float32)
    router_probs = jax.nn.softmax(logits, axis=-1)
    chosen = jnp.take_along_axis(router_probs, chosen_ids, axis=1)
    chosen_sum = jnp.sum(chosen, axis=1, keepdims=True)
    gate_vals = chosen / chosen_sum
    onehot = (
        chosen_ids.reshape(-1)[:, None] == jnp.arange(experts, dtype=jnp.int32)[None, :]
    ).astype(jnp.int32)
    rank_before = jnp.cumsum(onehot, axis=0) - onehot
    slot_pos = jnp.sum(rank_before * onehot, axis=1)
    slot_index = chosen_ids.reshape(-1) * capacity + slot_pos
    token_order = jnp.arange(tok_rows * top_count, dtype=jnp.int32) // top_count
    slot_token = (
        jnp.full((experts * capacity,), tok_rows, jnp.int32).at[slot_index].set(token_order)
    )
    grad_padded = jnp.concatenate(
        [upstream_grad, jnp.zeros((1, model_width), jnp.bfloat16)], axis=0
    )
    grad_slots = grad_padded[slot_token]
    gate_slots = (
        jnp.zeros((experts * capacity,), jnp.bfloat16)
        .at[slot_index]
        .set(gate_vals.reshape(-1).astype(jnp.bfloat16))
    )
    chosen_count = jnp.sum(onehot.reshape(tok_rows, top_count, experts), axis=1).astype(jnp.float32)
    local_counts = jnp.sum(chosen_count, axis=0)
    seq_counts = lax.psum(local_counts, "seq")
    recv_grad, recv_gate = (
        lax.all_to_all(
            grad_slots.reshape(experts, 1, capacity, model_width),
            ("seq", "exp"),
            split_axis=0,
            concat_axis=1,
            tiled=True,
        ),
        lax.all_to_all(
            gate_slots.reshape(experts, 1, capacity),
            ("seq", "exp"),
            split_axis=0,
            concat_axis=1,
            tiled=True,
        ),
    )
    back_rows, slot_combine = expert_backward(
        recv_grad.reshape(-1, model_width),
        recv_gate.reshape(-1),
        gate_weight[0],
        up_weight[0],
        down_weight[0],
        saved_gate[0],
        saved_up[0],
    )
    returned, combine_back = (
        lax.all_to_all(
            back_rows.reshape(1, devices, capacity, model_width),
            ("seq", "exp"),
            split_axis=1,
            concat_axis=0,
            tiled=True,
        ),
        lax.all_to_all(
            slot_combine.reshape(1, devices, capacity),
            ("seq", "exp"),
            split_axis=1,
            concat_axis=0,
            tiled=True,
        ),
    )
    returned_rows = returned.reshape(experts * capacity, model_width)
    expert_sum = jnp.sum(
        returned_rows[slot_index].reshape(tok_rows, top_count, model_width).astype(jnp.float32),
        axis=1,
    )
    combine_grad = (
        combine_back.reshape(-1)[slot_index].reshape(tok_rows, top_count).astype(jnp.float32)
    )
    prob_sel = (
        combine_grad - jnp.sum(gate_vals * combine_grad, axis=1, keepdims=True)
    ) / chosen_sum
    prob_grad = jnp.einsum(
        "tk,tke->te", prob_sel, onehot.reshape(tok_rows, top_count, experts).astype(jnp.float32)
    )
    fraction = experts * seq_counts / (top_count * tok_rows * seq_size)
    prob_grad = prob_grad + aux_weight[0] * fraction[None, :]
    dlogits = router_probs * (prob_grad - jnp.sum(router_probs * prob_grad, axis=1, keepdims=True))
    logit_grad = dlogits.astype(jnp.bfloat16)
    token_grad = expert_sum + jnp.einsum(
        "te,de->td", logit_grad, router_weight, preferred_element_type=jnp.float32
    )
    router_grad = lax.psum_scatter(
        jnp.einsum("td,te->de", inputs, logit_grad, preferred_element_type=jnp.float32),
        ("seq", "exp"),
        scatter_dimension=0,
        tiled=True,
    )
    return (token_grad.astype(jnp.bfloat16)[None], combine_grad[None], router_grad)


def solution(mesh):
    placed = (
        P("exp", "seq", None),
        P("exp", "seq", None),
        P(),
        P(("seq", "exp"), None, None),
        P(("seq", "exp"), None, None),
        P(("seq", "exp"), None, None),
        P(("seq", "exp"), None, None),
        P(("seq", "exp"), None, None),
        P("exp", "seq", None),
        P(),
    )
    return jax.shard_map(
        shards,
        mesh=mesh,
        in_specs=placed,
        out_specs=(P("exp", "seq", None), P("exp", "seq", None), P(("seq", "exp"), None)),
        check_vma=False,
    )
```

profile of v0, /device:TPU:0, one launch (start us, length us, event | category | flops | bytes accessed | tf_op | source)
XLA Modules:
  0.0 1073.2 jit_solution(6550109645006879006)
XLA Ops:
  9.6 9.0 reduce-window.6
  19.3 1.4 fusion.47
  21.6 7.0 gather_fusion.3
  29.1 7.6 scatter_custom_fusion
  37.4 7.3 all-to-all-start
  44.7 4.3 scatter_custom_fusion.1
  49.2 14.3 %gather_fusion = bf16[2048,4096]{1,0:T(8,128)(2,1)} fusion(bf16[129,4096]{1,0:T(8,128)(2,1)S(1)} %concatenate.3, s32[2048]{0:T(1024)S(1)} %fusion.33), kind=kCustom, calls=%fused_computation | custom fusion | bytes 33562624 | tf_op jit(solution)/shard_map/gather | solution.py:67
  63.5 6.4 all-to-all-start.1
  69.9 4.7 copy.63
  74.6 4.7 copy.62
  79.5 356.0 %all-to-all-done.1 = bf16[32,1,64,4096]{3,2,1,0:T(8,128)(2,1)} async-done(((bf16[32,1,64,4096]{3,2,1,0:T(8,128)(2,1)}), bf16[32,1,64,4096]{3,2,1,0:T(8,128)(2,1)}, u32[]{:S(2)}, u32[]{:S(2)}) %all-to-all-start.1) | async-done | bytes 16777248 | tf_op jit(solution)/shard_map/all_to_all | solution.py:77
  435.5 22.5 %fusion.4 = (bf16[2048]{0:T(1024)(128)(2,1)S(1)}, f32[2048,768]{0,1:T(8,128)}) fusion(bf16[1,2048,768]{1,2,0:T(8,128)(2,1)} %copy.62, bf16[1,2048,768]{1,2,0:T(8,128)(2,1)} %copy.63, bf16[2048,4096]{1,0:T(8,128)(2,1)} %bitcast.10, bf16[1,768,4096]{2,1,0:T(8,128)(2,1)} %param.15), kind=kOutput, calls=%fused_computation.17 | convolution fusion | flops 12899055616 | bytes 35655680 | tf_op jit(solution)/shard_map/rd,fd->rf/dot_general | solution.py:8
  458.7 16.5 %all-to-all-start.3 = ((bf16[1,32,64]{2,0,1:T(2,128)(2,1)}), bf16[1,32,64]{2,0,1:T(2,128)(2,1)S(1)}, u32[]{:S(2)}, u32[]{:S(2)}) async-start(bf16[1,32,64]{2,0,1:T(2,128)(2,1)} %convert_element_type.124), calls=%async_computation.3 | async-start | bytes 32768 | tf_op jit(solution)/shard_map/all_to_all | solution.py:109
  475.2 29.5 %fusion.10 = f32[2048,4096]{1,0:T(8,128)} fusion(bf16[1,4096,768]{2,1,0:T(8,128)(2,1)} %param.13, f32[2048,768]{0,1:T(8,128)} %get-tuple-element.18, bf16[1,2048,768]{1,2,0:T(8,128)(2,1)} %copy.62, bf16[1,2048,768]{1,2,0:T(8,128)(2,1)} %copy.63, f32[2048]{0:T(1024)S(1)} %reshape.193), kind=kOutput, calls=%fused_computation.23 | convolution fusion | flops 12905349120 | bytes 52436992 | tf_op jit(solution)/shard_map/rf,df->rd/dot_general | solution.py:20
  504.7 27.9 %add_convert_fusion = bf16[2048,4096]{1,0:T(8,128)(2,1)} fusion(f32[2048,4096]{1,0:T(8,128)} %fusion.10, bf16[1,4096,768]{2,1,0:T(8,128)(2,1)} %param.14, f32[2048,768]{0,1:T(8,128)} %get-tuple-element.18, f32[2048]{0:T(1024)S(1)} %reshape.193, bf16[1,2048,768]{1,2,0:T(8,128)(2,1)} %copy.63), kind=kOutput, calls=%fused_computation.6 | convolution fusion | flops 12914262016 | bytes 66068480 | tf_op jit(solution)/shard_map/rf,df->rd/dot_general | solution.py:21
  532.6 6.1 all-to-all-start.2
  539.6 290.8 %psum.7 = f32[32]{0:T(128)S(1)} all-reduce(f32[32]{0:T(128)S(1)} %convert_reduce_fusion.3), channel_id=1, replica_groups=mesh['seq'=8,'exp'=4] {'seq'}, use_global_device_ids=true, to_apply=%region_13.14 | all-reduce | flops 32 | bytes 256 | tf_op jit(solution)/shard_map/psum | solution.py:75
  830.5 6.8 gather_fusion.2
  838.0 1.1 convolution_bitcast_fusion
  839.9 64.5 %all-to-all-done.2 = bf16[1,32,64,4096]{3,2,0,1:T(8,128)(2,1)} async-done(((bf16[1,32,64,4096]{3,2,0,1:T(8,128)(2,1)}), bf16[1,32,64,4096]{3,2,0,1:T(8,128)(2,1)}, u32[]{:S(2)}, u32[]{:S(2)}) %all-to-all-start.2) | async-done | bytes 16777248 | tf_op jit(solution)/shard_map/all_to_all | solution.py:102
  904.4 23.0 %gather_fusion.1 = bf16[1024,4096]{1,0:T(8,128)(2,1)} fusion(bf16[2048,4096]{1,0:T(8,128)(2,1)} %bitcast.19, s32[1024]{0:T(1024)S(1)} %broadcast_clamp_fusion), kind=kCustom, calls=%fused_computation.1 | custom fusion | bytes 16781312 | tf_op jit(solution)/shard_map/gather | solution.py:119
  927.4 9.1 convert_reduce_fusion
  936.5 1.4 fusion.15
  937.9 128.2 %reduce-scatter.2.cloned.1.call-done = f32[128,32]{0,1:T(8,128)} async-done(((f32[4096,32]{0,1:T(8,128)}), f32[128,32]{0,1:T(8,128)}) %reduce-scatter.2.cloned.1.call-update) | async-done | bytes 16400 | tf_op jit(solution)/shard_map/reduce_scatter | solution.py:138
  (71 shorter events, 7.7 us)
Async XLA Ops:
  7.2 12.1 %copy-start = (bf16[1,128,4096]{2,1,0:T(8,128)(2,1)S(1)}, bf16[1,128,4096]{2,1,0:T(8,128)(2,1)}, u32[]{:S(2)}) copy-start(bf16[1,128,4096]{2,1,0:T(8,128)(2,1)} %param.10) | copy-start | bytes 3145732
  20.7 0.6 copy-start.3
  20.8 7.8 copy-start.6
  20.8 7.8 copy-start.8
  21.5 27.5 %copy-start.1 = (bf16[1,128,4096]{2,1,0:T(8,128)(2,1)S(1)}, bf16[1,128,4096]{2,1,0:T(8,128)(2,1)}, u32[]{:S(2)}) copy-start(bf16[1,128,4096]{2,1,0:T(8,128)(2,1)} %param.11) | copy-start | bytes 3145732
  37.4 26.1 %all-to-all-start = ((bf16[32,1,64]{2,1,0:T(2,128)(2,1)}), bf16[32,1,64]{2,1,0:T(2,128)(2,1)S(1)}, u32[]{:S(2)}, u32[]{:S(2)}) async-start(bf16[32,1,64]{2,1,0:T(2,128)(2,1)} %reshape.249), calls=%async_computation | async-start | bytes 32768 | tf_op jit(solution)/shard_map/all_to_all | solution.py:84
  63.5 372.0 %all-to-all-start.1 = ((bf16[32,1,64,4096]{3,2,1,0:T(8,128)(2,1)}), bf16[32,1,64,4096]{3,2,1,0:T(8,128)(2,1)}, u32[]{:S(2)}, u32[]{:S(2)}) async-start(bf16[32,1,64,4096]{3,2,1,0:T(8,128)(2,1)} %bitcast.92), calls=%async_computation.1 | async-start | bytes 33554432 | tf_op jit(solution)/shard_map/all_to_all | solution.py:77
  458.7 73.9 %all-to-all-start.3 = ((bf16[1,32,64]{2,0,1:T(2,128)(2,1)}), bf16[1,32,64]{2,0,1:T(2,128)(2,1)S(1)}, u32[]{:S(2)}, u32[]{:S(2)}) async-start(bf16[1,32,64]{2,0,1:T(2,128)(2,1)} %convert_element_type.124), calls=%async_computation.3 | async-start | bytes 32768 | tf_op jit(solution)/shard_map/all_to_all | solution.py:109
  532.6 6.8 copy-start.5
  532.6 305.2 %copy-start.4 = (f32[128,32]{0,1:T(8,128)S(1)}, f32[128,32]{0,1:T(8,128)}, u32[]{:S(2)}) copy-start(f32[128,32]{0,1:T(8,128)} %copy-done.3) | copy-start | bytes 49156
  532.6 305.2 %copy-start.7 = (f32[128]{0:T(128)S(1)}, f32[128]{0:T(128)}, u32[]{:S(2)}) copy-start(f32[128]{0:T(128)} %copy-done.6) | copy-start | bytes 1540
  532.6 305.2 %copy-start.9 = (f32[128]{0:T(128)S(1)}, f32[128]{0:T(128)}, u32[]{:S(2)}) copy-start(f32[128]{0:T(128)} %copy-done.8) | copy-start | bytes 1540
  532.6 371.7 %all-to-all-start.2 = ((bf16[1,32,64,4096]{3,2,0,1:T(8,128)(2,1)}), bf16[1,32,64,4096]{3,2,0,1:T(8,128)(2,1)}, u32[]{:S(2)}, u32[]{:S(2)}) async-start(bf16[1,32,64,4096]{3,2,0,1:T(8,128)(2,1)} %bitcast.93), calls=%async_computation.2 | async-start | bytes 33554432 | tf_op jit(solution)/shard_map/all_to_all | solution.py:102
  538.7 527.4 %reduce-scatter.2.cloned.1.call-start = ((), (), s32[]{:S(2)}) async-start(), calls=%async_computation.5 | async-start | bytes 540672 | tf_op jit(solution)/shard_map/reduce_scatter | solution.py:138
  927.4 9.1 copy-start.2
Sparse Core Ops, SparseCore 0:
  839.3 226.7 reduce-scatter.1
where the time goes:
time: 1080 us; the launch traced here: 1070 us
  waiting for transfers between devices  549 us (51%)
  blocking collectives  291 us (27%)
  matrix products  83.9 us (8%)
  local copies, waits for them, and re-layouts  77.6 us (7%)
  starting transfers between devices  36.4 us (3%)
  other arithmetic  20.6 us (2%)
  between operations  15.3 us (1%)
    all_to_all x1, waiting for transfers between devices, shards(): lax.all_to_all(grad_slots.reshape(experts, 1, capacity, model_width), ('s...  356 us
    psum x1, blocking collectives, shards(): seq_counts = lax.psum(local_counts, 'seq')  291 us
    reduce_scatter x1, waiting for transfers between devices, shards(): lax.psum_scatter(jnp.einsum('td,te->de', inputs, logit_grad, preferred_el...  128 us
    all_to_all x1, waiting for transfers between devices, shards(): lax.all_to_all(back_rows.reshape(1, devices, capacity, model_width), ('se...  64.5 us
    dot_general x1, matrix products, expert_backward(): jnp.einsum('rf,df->rd', grad_first, w_gate, preferred_element_type=jnp.fl...  29.5 us
    dot_general x1, matrix products, expert_backward(): jnp.einsum('rf,df->rd', grad_second, w_up, preferred_element_type=jnp.flo...  27.9 us
    gather x1, local copies, waits for them, and re-layouts, shards(): returned_rows[slot_index].reshape(tok_rows, top_count, model_width)  23 us
    dot_general x1, matrix products, expert_backward(): jnp.einsum('rd,fd->rf', grad_rows, w_down, preferred_element_type=jnp.flo...  22.5 us
  transfers between devices with their start and end apart: 5, of which 3 were waited for; matrix products, arithmetic and copies ran while one was open for 12% of the time, Pallas kernels for 0%

commit v1 on v0

--- a/solution.py
+++ b/solution.py
@@ -74,12 +74,20 @@
     local_counts = jnp.sum(chosen_count, axis=0)
     seq_counts = lax.psum(local_counts, "seq")
     recv_grad, recv_gate = (
-        lax.all_to_all(
-            grad_slots.reshape(experts, 1, capacity, model_width),
-            ("seq", "exp"),
-            split_axis=0,
-            concat_axis=1,
-            tiled=True,
+        jnp.concatenate(
+            lax.all_to_all(
+                jnp.stack(
+                    jnp.split(
+                        grad_slots.reshape(experts, 1, capacity, model_width),
+                        lax.axis_size(("seq", "exp")),
+                        axis=0,
+                    )
+                ),
+                ("seq", "exp"),
+                0,
+                0,
+            ),
+            axis=1,
         ),
         lax.all_to_all(
             gate_slots.reshape(experts, 1, capacity),

time: 1080 us -> 1140 us (1.056)
  local copies, waits for them, and re-layouts: 77.6 us -> 138 us
    unnamed x25 -> x72, local copies, waits for them, and re-layouts: 11.6 us -> 70.4 us
  transfers between devices with their start and end apart: 5 -> 5, of which waited for: 3 -> 3; matrix products, arithmetic and copies ran while one was open for 12% -> 17% of each run, Pallas kernels for 0% -> 0%
where the time goes in v1:
time: 1140 us; the launch traced here: 1130 us
  waiting for transfers between devices  549 us (48%)
  blocking collectives  291 us (26%)
  local copies, waits for them, and re-layouts  138 us (12%)
  matrix products  83.9 us (7%)
  starting transfers between devices  36.4 us (3%)
  other arithmetic  20.6 us (2%)
  between operations  15.4 us (1%)
    all_to_all x1, waiting for transfers between devices, shards(): lax.all_to_all(jnp.stack(jnp.split(grad_slots.reshape(experts, 1, capacit...  356 us
    psum x1, blocking collectives, shards(): seq_counts = lax.psum(local_counts, 'seq')  291 us
    reduce_scatter x1, waiting for transfers between devices, shards(): lax.psum_scatter(jnp.einsum('td,te->de', inputs, logit_grad, preferred_el...  128 us
    unnamed x72, local copies, waits for them, and re-layouts  70.4 us
    all_to_all x1, waiting for transfers between devices, shards(): lax.all_to_all(back_rows.reshape(1, devices, capacity, model_width), ('se...  64.5 us
    dot_general x1, matrix products, expert_backward(): jnp.einsum('rf,df->rd', grad_first, w_gate, preferred_element_type=jnp.fl...  29.5 us
    dot_general x1, matrix products, expert_backward(): jnp.einsum('rf,df->rd', grad_second, w_up, preferred_element_type=jnp.flo...  27.9 us
    gather x1, local copies, waits for them, and re-layouts, shards(): returned_rows[slot_index].reshape(tok_rows, top_count, model_width)  23 us
  transfers between devices with their start and end apart: 5, of which 3 were waited for; matrix products, arithmetic and copies ran while one was open for 17% of the time, Pallas kernels for 0%

profile of v1, /device:TPU:0, one launch (start us, length us, event | category | flops | bytes accessed | tf_op | source)
XLA Modules:
  0.0 1134.0 jit_solution(14907982485932970042)
XLA Ops:
  9.6 9.0 reduce-window.6
  21.5 7.0 gather_fusion.3
  29.4 7.6 scatter_custom_fusion
  37.7 7.3 all-to-all-start
  45.0 4.3 scatter_custom_fusion.1
  49.5 14.3 %gather_fusion = bf16[2048,4096]{1,0:T(8,128)(2,1)} fusion(bf16[129,4096]{1,0:T(8,128)(2,1)S(1)} %concatenate.3, s32[2048]{0:T(1024)S(1)} %fusion.65), kind=kCustom, calls=%fused_computation | custom fusion | bytes 33562624 | tf_op jit(solution)/shard_map/gather | solution.py:67
  93.9 1.9 fusion.40
  95.9 1.9 fusion.39
  111.0 1.9 fusion.31
  124.1 6.4 all-to-all-start.1
  130.6 4.7 copy.60
  135.3 4.7 copy.59
  140.1 356.0 %all-to-all-done.1 = bf16[32,1,1,64,4096]{4,3,2,1,0:T(8,128)(2,1)} async-done(((bf16[32,1,1,64,4096]{4,3,2,1,0:T(8,128)(2,1)}), bf16[32,1,1,64,4096]{4,3,2,1,0:T(8,128)(2,1)}, u32[]{:S(2)}, u32[]{:S(2)}) %all-to-all-start.1) | async-done | bytes 16777248 | tf_op jit(solution)/shard_map/all_to_all | solution.py:78
  496.1 22.5 %fusion.4 = (bf16[2048]{0:T(1024)(128)(2,1)S(1)}, f32[2048,768]{0,1:T(8,128)}) fusion(bf16[1,2048,768]{1,2,0:T(8,128)(2,1)} %copy.59, bf16[1,2048,768]{1,2,0:T(8,128)(2,1)} %copy.60, bf16[2048,4096]{1,0:T(8,128)(2,1)} %bitcast.40, bf16[1,768,4096]{2,1,0:T(8,128)(2,1)} %param.15), kind=kOutput, calls=%fused_computation.17 | convolution fusion | flops 12899055616 | bytes 35655680 | tf_op jit(solution)/shard_map/rd,fd->rf/dot_general | solution.py:8
  519.4 16.5 %all-to-all-start.3 = ((bf16[1,32,64]{2,0,1:T(2,128)(2,1)}), bf16[1,32,64]{2,0,1:T(2,128)(2,1)S(1)}, u32[]{:S(2)}, u32[]{:S(2)}) async-start(bf16[1,32,64]{2,0,1:T(2,128)(2,1)} %convert_element_type.124), calls=%async_computation.3 | async-start | bytes 32768 | tf_op jit(solution)/shard_map/all_to_all | solution.py:117
  535.9 29.5 %fusion.10 = f32[2048,4096]{1,0:T(8,128)} fusion(bf16[1,4096,768]{2,1,0:T(8,128)(2,1)} %param.13, f32[2048,768]{0,1:T(8,128)} %get-tuple-element.18, bf16[1,2048,768]{1,2,0:T(8,128)(2,1)} %copy.59, bf16[1,2048,768]{1,2,0:T(8,128)(2,1)} %copy.60, f32[2048]{0:T(1024)S(1)} %reshape.246), kind=kOutput, calls=%fused_computation.23 | convolution fusion | flops 12905349120 | bytes 52436992 | tf_op jit(solution)/shard_map/rf,df->rd/dot_general | solution.py:20
  565.4 27.9 %add_convert_fusion = bf16[2048,4096]{1,0:T(8,128)(2,1)} fusion(f32[2048,4096]{1,0:T(8,128)} %fusion.10, bf16[1,4096,768]{2,1,0:T(8,128)(2,1)} %param.14, f32[2048,768]{0,1:T(8,128)} %get-tuple-element.18, f32[2048]{0:T(1024)S(1)} %reshape.246, bf16[1,2048,768]{1,2,0:T(8,128)(2,1)} %copy.60), kind=kOutput, calls=%fused_computation.6 | convolution fusion | flops 12914262016 | bytes 66068480 | tf_op jit(solution)/shard_map/rf,df->rd/dot_general | solution.py:21
  593.3 6.1 all-to-all-start.2
  600.3 290.8 %psum.7 = f32[32]{0:T(128)S(1)} all-reduce(f32[32]{0:T(128)S(1)} %convert_reduce_fusion.3), channel_id=1, replica_groups=mesh['seq'=8,'exp'=4] {'seq'}, use_global_device_ids=true, to_apply=%region_13.14 | all-reduce | flops 32 | bytes 256 | tf_op jit(solution)/shard_map/psum | solution.py:75
  891.2 6.8 gather_fusion.2
  900.6 64.5 %all-to-all-done.2 = bf16[1,32,64,4096]{3,2,0,1:T(8,128)(2,1)} async-done(((bf16[1,32,64,4096]{3,2,0,1:T(8,128)(2,1)}), bf16[1,32,64,4096]{3,2,0,1:T(8,128)(2,1)}, u32[]{:S(2)}, u32[]{:S(2)}) %all-to-all-start.2) | async-done | bytes 16777248 | tf_op jit(solution)/shard_map/all_to_all | solution.py:110
  965.1 23.0 %gather_fusion.1 = bf16[1024,4096]{1,0:T(8,128)(2,1)} fusion(bf16[2048,4096]{1,0:T(8,128)(2,1)} %bitcast.49, s32[1024]{0:T(1024)S(1)} %broadcast_clamp_fusion), kind=kCustom, calls=%fused_computation.1 | custom fusion | bytes 16781312 | tf_op jit(solution)/shard_map/gather | solution.py:127
  988.1 9.1 convert_reduce_fusion
  998.6 128.3 %reduce-scatter.2.cloned.1.call-done = f32[128,32]{0,1:T(8,128)} async-done(((f32[4096,32]{0,1:T(8,128)}), f32[128,32]{0,1:T(8,128)}) %reduce-scatter.2.cloned.1.call-update) | async-done | bytes 16400 | tf_op jit(solution)/shard_map/reduce_scatter | solution.py:146
  (119 shorter events, 66.4 us)
Async XLA Ops:
  7.2 12.2 %copy-start = (bf16[1,128,4096]{2,1,0:T(8,128)(2,1)S(1)}, bf16[1,128,4096]{2,1,0:T(8,128)(2,1)}, u32[]{:S(2)}) copy-start(bf16[1,128,4096]{2,1,0:T(8,128)(2,1)} %param.10) | copy-start | bytes 3145732
  8.1 20.6 %copy-start.1 = (s32[1,128,8]{2,1,0:T(8,128)}, s32[1,128,8]{2,1,0:T(8,128)S(1)}, u32[]{:S(2)}) copy-start(s32[1,128,8]{2,1,0:T(8,128)S(1)} %copy.52) | copy-start | bytes 12292
  20.7 0.6 copy-start.7
  20.8 7.7 copy-start.12
  20.8 7.7 copy-start.16
  21.5 27.9 %copy-start.3 = (bf16[1,128,4096]{2,1,0:T(8,128)(2,1)S(1)}, bf16[1,128,4096]{2,1,0:T(8,128)(2,1)}, u32[]{:S(2)}) copy-start(bf16[1,128,4096]{2,1,0:T(8,128)(2,1)} %param.11) | copy-start | bytes 3145732
  28.6 20.8 %copy-start.5 = (f32[128,8]{1,0:T(8,128)}, f32[128,8]{1,0:T(8,128)S(1)}, u32[]{:S(2)}) copy-start(f32[128,8]{1,0:T(8,128)S(1)} %reshape.279) | copy-start | bytes 12292
  28.7 0.6 copy-start.14
  29.4 20.0 %copy-start.10 = (s32[1024,1]{0,1:T(1,128)}, s32[1024,1]{0,1:T(1,128)S(1)}, u32[]{:S(2)}) copy-start(s32[1024,1]{0,1:T(1,128)S(1)} %compare_select_fusion.1) | copy-start | bytes 12292
  37.7 86.4 %all-to-all-start = ((bf16[32,1,64]{2,1,0:T(2,128)(2,1)}), bf16[32,1,64]{2,1,0:T(2,128)(2,1)S(1)}, u32[]{:S(2)}, u32[]{:S(2)}) async-start(bf16[32,1,64]{2,1,0:T(2,128)(2,1)} %reshape.302), calls=%async_computation | async-start | bytes 32768 | tf_op jit(solution)/shard_map/all_to_all | solution.py:92
  124.1 372.0 %all-to-all-start.1 = ((bf16[32,1,1,64,4096]{4,3,2,1,0:T(8,128)(2,1)}), bf16[32,1,1,64,4096]{4,3,2,1,0:T(8,128)(2,1)}, u32[]{:S(2)}, u32[]{:S(2)}) async-start(bf16[32,1,1,64,4096]{4,3,2,1,0:T(8,128)(2,1)} %fusion.25), calls=%async_computation.1 | async-start | bytes 33554432 | tf_op jit(solution)/shard_map/all_to_all | solution.py:78
  519.4 73.9 %all-to-all-start.3 = ((bf16[1,32,64]{2,0,1:T(2,128)(2,1)}), bf16[1,32,64]{2,0,1:T(2,128)(2,1)S(1)}, u32[]{:S(2)}, u32[]{:S(2)}) async-start(bf16[1,32,64]{2,0,1:T(2,128)(2,1)} %convert_element_type.124), calls=%async_computation.3 | async-start | bytes 32768 | tf_op jit(solution)/shard_map/all_to_all | solution.py:117
  593.3 6.9 copy-start.9
  593.3 297.8 %copy-start.11 = (s32[1024,1]{0,1:T(1,128)S(1)}, s32[1024,1]{0,1:T(1,128)}, u32[]{:S(2)}) copy-start(s32[1024,1]{0,1:T(1,128)} %copy-done.10) | copy-start | bytes 12292
  593.3 304.8 %copy-start.2 = (s32[1,128,8]{2,1,0:T(8,128)S(1)}, s32[1,128,8]{2,1,0:T(8,128)}, u32[]{:S(2)}) copy-start(s32[1,128,8]{2,1,0:T(8,128)} %copy-done.1) | copy-start | bytes 12292
  593.3 304.8 %copy-start.6 = (f32[128,8]{1,0:T(8,128)S(1)}, f32[128,8]{1,0:T(8,128)}, u32[]{:S(2)}) copy-start(f32[128,8]{1,0:T(8,128)} %copy-done.5) | copy-start | bytes 12292
  593.3 304.8 %copy-start.15 = (f32[128]{0:T(128)S(1)}, f32[128]{0:T(128)}, u32[]{:S(2)}) copy-start(f32[128]{0:T(128)} %copy-done.14) | copy-start | bytes 1540
  593.3 305.2 %copy-start.8 = (f32[128,32]{0,1:T(8,128)S(1)}, f32[128,32]{0,1:T(8,128)}, u32[]{:S(2)}) copy-start(f32[128,32]{0,1:T(8,128)} %copy-done.7) | copy-start | bytes 49156
  593.3 305.2 %copy-start.13 = (f32[128]{0:T(128)S(1)}, f32[128]{0:T(128)}, u32[]{:S(2)}) copy-start(f32[128]{0:T(128)} %copy-done.12) | copy-start | bytes 1540
  593.3 305.2 %copy-start.17 = (f32[128]{0:T(128)S(1)}, f32[128]{0:T(128)}, u32[]{:S(2)}) copy-start(f32[128]{0:T(128)} %copy-done.16) | copy-start | bytes 1540
  593.3 371.7 %all-to-all-start.2 = ((bf16[1,32,64,4096]{3,2,0,1:T(8,128)(2,1)}), bf16[1,32,64,4096]{3,2,0,1:T(8,128)(2,1)}, u32[]{:S(2)}, u32[]{:S(2)}) async-start(bf16[1,32,64,4096]{3,2,0,1:T(8,128)(2,1)} %bitcast.217), calls=%async_computation.2 | async-start | bytes 33554432 | tf_op jit(solution)/shard_map/all_to_all | solution.py:110
  599.4 527.5 %reduce-scatter.2.cloned.1.call-start = ((), (), s32[]{:S(2)}) async-start(), calls=%async_computation.5 | async-start | bytes 540672 | tf_op jit(solution)/shard_map/reduce_scatter | solution.py:146
  965.1 32.1 %copy-start.4 = (bf16[4096,32]{0,1:T(8,128)(2,1)S(1)}, bf16[4096,32]{0,1:T(8,128)(2,1)}, u32[]{:S(2)}) copy-start(bf16[4096,32]{0,1:T(8,128)(2,1)} %param.12) | copy-start | bytes 786436
Sparse Core Ops, SparseCore 0:
  900.0 226.8 reduce-scatter.1
